TPU v7x, 128 devices: a whole 4x4x4 slice. The times are simulated.
128 devices in a mesh: col: 16 (over y, z), row: 8 (over x, core).
Axes of the slice: x: 4, y: 4, z: 4, core: 2. Of those that a mesh axis runs over, the one named last changes fastest.
Arguments:
- u_factors: bfloat16 [2, 64, 256, 64, 128], P(None, 'row', None, 'col'), may hold values from -0.09375 to 0.09375
- v_factors: bfloat16 [2, 64, 256, 64, 128], P(None, 'row', None, 'col'), may hold values from -0.375 to 0.375
- ranks: int32 [2, 64, 64], P(None, 'row', 'col'), may hold values from 8 to 64
- model_init: float32 [2, 16384, 256], P(None, ('col', 'row')), may hold values from -6 to 6
- observed: float32 [2, 16384, 256], P(None, ('row', 'col')), may hold values from -6 to 6
- step: float32 [2], replicated, may hold values from 0.1 to 0.4
Outputs:
- model: float32 [2, 16384, 256], P(None, ('col', 'row'))
- misfit: float32 [2, 16384, 256], P(None, ('row', 'col'))
Inputs may be any that keep to these rules, and one draw needn't show every extreme that they name: `ranks`: columns of a factor beyond its tile's rank do not count.
All inputs are finite; a program needn't handle non-finite values.
Results may differ from a plain program's by a relative error of at most 0.0085.
Values may be sent and summed in bfloat16 or wider, within the bound.
A program may use at most 128 MiB of HBM per device.

v0:
```python
import jax
import jax.numpy as jnp
from jax import lax
from jax.sharding import PartitionSpec as P

ITERS = 2


def split_product(product, rank_mask, rank_most, right_count):
    real = product[..., :rank_most, :right_count] + product[..., rank_most:, right_count:]
    imaginary = product[..., :rank_most, right_count:] - product[..., rank_most:, :right_count]
    weights = rank_mask[..., None]
    return jnp.concatenate([real * weights, imaginary * weights], -1).astype(jnp.bfloat16)


def expand_complex(coefficient, right_count):
    real = coefficient[..., :right_count]
    imaginary = coefficient[..., right_count:]
    upper = jnp.concatenate([real, imaginary], -1)
    lower = jnp.concatenate([-imaginary, real], -1)
    return jnp.concatenate([upper, lower], -2)


def local(u_factors, v_factors, ranks, model_init, observed, step):
    frequencies = model_init.shape[0]
    rank_most = u_factors.shape[-1] // 2
    right_count = model_init.shape[-1] // 2
    tile_size = u_factors.shape[2]
    rows_here = u_factors.shape[1]
    cols_here = u_factors.shape[3]
    rank_mask = (
        jnp.arange(rank_most, dtype=jnp.int32)[None, None, None, :] < ranks[..., None]
    ).astype(jnp.float32)
    model = model_init
    misfit = model_init
    observed_block = lax.all_gather(observed, "col", axis=1, tiled=True)
    for sweep in range(ITERS):
        gathered = lax.all_gather(model.astype(jnp.bfloat16), "row", axis=1, tiled=True)
        model_tiles = gathered.reshape(frequencies, cols_here, tile_size, 2 * right_count)
        product = jnp.einsum(
            "fiajk,fjal->fijkl", v_factors, model_tiles, preferred_element_type=jnp.float32
        )
        coefficient = expand_complex(
            split_product(product, rank_mask, rank_most, right_count), right_count
        )
        partial_value = jnp.einsum(
            "fiajk,fijkl->fial", u_factors, coefficient, preferred_element_type=jnp.float32
        )
        partial_value = partial_value.reshape(frequencies, rows_here * tile_size, 2 * right_count)
        predicted = lax.psum(partial_value, "col")
        full_misfit = predicted - observed_block
        misfit_half = full_misfit.astype(jnp.bfloat16)
        share = observed.shape[1]
        misfit = lax.dynamic_slice_in_dim(full_misfit, lax.axis_index("col") * share, share, 1)
        misfit_tiles = misfit_half.reshape(frequencies, rows_here, tile_size, 2 * right_count)
        product = jnp.einsum(
            "fiajk,fial->fijkl", u_factors, misfit_tiles, preferred_element_type=jnp.float32
        )
        back = expand_complex(
            split_product(product, rank_mask, rank_most, right_count), right_count
        )
        gradient_part = jnp.einsum(
            "fiajk,fijkl->fjal", v_factors, back, preferred_element_type=jnp.float32
        )
        gradient_part = gradient_part.reshape(frequencies, cols_here * tile_size, 2 * right_count)
        gradient = lax.psum_scatter(gradient_part, "row", scatter_dimension=1, tiled=True)
        model = model - step[:, None, None] * gradient
    return (model, misfit)


def solution(mesh):
    return jax.shard_map(
        local,
        mesh=mesh,
        in_specs=(
            P(None, "row", None, "col", None),
            P(None, "row", None, "col", None),
            P(None, "row", "col"),
            P(None, ("col", "row"), None),
            P(None, ("row", "col"), None),
            P(),
        ),
        out_specs=(P(None, ("col", "row"), None), P(None, ("row", "col"), None)),
        check_vma=False,
    )
```

profile of v0, /device:TPU:0, one launch (start us, length us, event | category | flops | bytes accessed | tf_op | source)
XLA Modules:
  0.0 443.3 jit_solution(17294954381206863518)
XLA Ops:
  7.2 1.6 convert_element_type.23
  8.9 7.5 %copy.8 = bf16[2,8,256,4,128]{2,4,1,3,0:T(8,128)(2,1)} copy(bf16[2,8,256,4,128]{4,3,2,1,0:T(4,128)(2,1)} %param.7) | data formatting | bytes 8388608 | tf_op args[1]
  16.4 7.4 %copy.11 = bf16[2,8,256,4,128]{2,4,3,1,0:T(8,128)(2,1)} copy(bf16[2,8,256,4,128]{4,3,2,1,0:T(4,128)(2,1)} %param.6) | data formatting | bytes 8388608 | tf_op args[0]
  23.8 12.1 %all-gather.4.cloned.1.call-done = bf16[2,1024,256]{2,1,0:T(8,128)(2,1)} async-done(((bf16[2,128,256]{2,1,0:T(8,128)(2,1)}), bf16[2,1024,256]{2,1,0:T(8,128)(2,1)}) %all-gather.4.cloned.1.call-update) | async-done | bytes 1048592 | tf_op jit(solution)/shard_map/all_gather | solution.py:38
  36.0 3.7 fusion.49
  41.2 1.5 copy-done
  42.7 2.9 fusion.18
  46.4 103.1 %all-reduce.3.cloned.1.call-done = f32[2,2048,256]{2,1,0:T(8,128)} async-done(((f32[2,2048,256]{2,1,0:T(8,128)}), f32[2,2048,256]{2,1,0:T(8,128)}) %all-reduce.3.cloned.1.call-update) | async-done | bytes 4194320 | tf_op jit(solution)/shard_map/psum | solution.py:50
  149.5 53.4 %all-gather.6.cloned.1.call-done = f32[2,2048,256]{2,1,0:T(8,128)} async-done(((f32[2,128,256]{2,1,0:T(8,128)}), f32[2,2048,256]{2,1,0:T(8,128)}) %all-gather.6.cloned.1.call-update) | async-done | bytes 4194320 | tf_op jit(solution)/shard_map/all_gather | solution.py:36
  202.9 4.3 subtract_convert_fusion
  211.3 1.5 copy-done.4
  212.8 2.8 fusion
  215.6 33.5 %reduce-scatter.3.cloned.1.call-done = f32[2,128,256]{2,1,0:T(8,128)} async-done(((f32[2,1024,256]{2,1,0:T(8,128)}), f32[2,128,256]{2,1,0:T(8,128)}) %reduce-scatter.3.cloned.1.call-update) | async-done | bytes 262160 | tf_op jit(solution)/shard_map/reduce_scatter | solution.py:66
  249.1 1.7 fusion.36
  250.9 22.4 %all-gather.8.cloned.1.call-done = bf16[2,1024,256]{2,1,0:T(8,128)(2,1)} async-done(((bf16[2,128,256]{2,1,0:T(8,128)(2,1)}), bf16[2,1024,256]{2,1,0:T(8,128)(2,1)}) %all-gather.8.cloned.1.call-update) | async-done | bytes 1048592 | tf_op jit(solution)/shard_map/all_gather | solution.py:38
  273.3 3.7 fusion.51
  278.6 1.5 copy-done.2
  280.0 2.9 fusion.16
  283.2 103.7 %all-reduce.5.cloned.1.call-done = f32[2,2048,256]{2,1,0:T(8,128)} async-done(((f32[2,2048,256]{2,1,0:T(8,128)}), f32[2,2048,256]{2,1,0:T(8,128)}) %all-reduce.5.cloned.1.call-update) | async-done | bytes 4194320 | tf_op jit(solution)/shard_map/psum | solution.py:50
  386.8 6.2 %fusion.42 = (bf16[2,2048,256]{2,1,0:T(8,128)(2,1)S(1)}, f32[2,2048,256]{2,1,0:T(8,128)}) fusion(f32[2,2048,256]{2,1,0:T(8,128)} %all-reduce.5.cloned.1.call-done, f32[2,2048,256]{2,1,0:T(8,128)} %all-gather.6.cloned.1.call-done), kind=kLoop, calls=%fused_computation.58 | loop fusion | flops 2097152 | bytes 14680064 | tf_op jit(solution)/shard_map/convert_element_type | solution.py:52
  398.3 2.8 fusion.8
  401.1 1.7 constant_dynamic-slice_fusion
  402.7 32.0 %reduce-scatter.5.cloned.1.call-done = f32[2,128,256]{2,1,0:T(8,128)} async-done(((f32[2,1024,256]{2,1,0:T(8,128)}), f32[2,128,256]{2,1,0:T(8,128)}) %reduce-scatter.5.cloned.1.call-update) | async-done | bytes 262160 | tf_op jit(solution)/shard_map/reduce_scatter | solution.py:66
  434.7 1.8 multiply_subtract_fusion
  (44 shorter events, 13.6 us)
Async XLA Ops:
  7.2 28.8 %all-gather.4.cloned.1.call-start = ((), (), s32[]{:S(2)}) async-start(), calls=%async_computation.2 | async-start | bytes 1179648 | tf_op jit(solution)/shard_map/all_gather | solution.py:38
  8.9 140.7 %all-reduce.3.cloned.1.call-start = ((), (), s32[]{:S(2)}) async-start(), calls=%async_computation.3 | async-start | bytes 8388608 | tf_op jit(solution)/shard_map/psum | solution.py:50
  16.4 7.4 %copy-start.8 = (s32[2,8,4]{1,2,0:T(4,128)S(1)}, s32[2,8,4]{1,2,0:T(4,128)}, u32[]{:S(2)}) copy-start(s32[2,8,4]{1,2,0:T(4,128)} %param.8) | copy-start | bytes 772
  40.5 2.2 copy-start
  45.6 157.3 %all-gather.6.cloned.1.call-start = ((), (), s32[]{:S(2)}) async-start(), calls=%async_computation.4 | async-start | bytes 4456448 | tf_op jit(solution)/shard_map/all_gather | solution.py:36
  46.4 202.7 %reduce-scatter.3.cloned.1.call-start = ((), (), s32[]{:S(2)}) async-start(), calls=%async_computation.5 | async-start | bytes 2359296 | tf_op jit(solution)/shard_map/reduce_scatter | solution.py:66
  202.9 4.6 %copy-start.1 = (bf16[2,8,256,4,128]{2,4,3,1,0:T(8,128)(2,1)S(1)}, bf16[2,8,256,4,128]{2,4,3,1,0:T(8,128)(2,1)}, u32[]{:S(2)}) copy-start(bf16[2,8,256,4,128]{2,4,3,1,0:T(8,128)(2,1)} %copy.11) | copy-start | bytes 12582916
  210.6 2.2 copy-start.4
  212.8 36.3 %copy-start.6 = (f32[2,128,256]{2,1,0:T(8,128)S(1)}, f32[2,128,256]{2,1,0:T(8,128)}, u32[]{:S(2)}) copy-start(f32[2,128,256]{2,1,0:T(8,128)} %param.9) | copy-start | bytes 786436
  212.8 36.3 %copy-start.9 = (f32[2]{0:T(128)S(1)}, f32[2]{0:T(128)}, u32[]{:S(2)}) copy-start(f32[2]{0:T(128)} %param.11) | copy-start | bytes 28
  215.6 57.7 %all-gather.8.cloned.1.call-start = ((), (), s32[]{:S(2)}) async-start(), calls=%async_computation.6 | async-start | bytes 1179648 | tf_op jit(solution)/shard_map/all_gather | solution.py:38
  250.8 136.0 %all-reduce.5.cloned.1.call-start = ((), (), s32[]{:S(2)}) async-start(), calls=%async_computation.7 | async-start | bytes 8388608 | tf_op jit(solution)/shard_map/psum | solution.py:50
  277.8 2.2 copy-start.2
  283.0 151.8 %reduce-scatter.5.cloned.1.call-start = ((), (), s32[]{:S(2)}) async-start(), calls=%async_computation.8 | async-start | bytes 2359296 | tf_op jit(solution)/shard_map/reduce_scatter | solution.py:66
  386.8 6.2 %copy-start.3 = (bf16[2,8,256,4,128]{2,4,3,1,0:T(8,128)(2,1)S(1)}, bf16[2,8,256,4,128]{2,4,3,1,0:T(8,128)(2,1)}, u32[]{:S(2)}) copy-start(bf16[2,8,256,4,128]{2,4,3,1,0:T(8,128)(2,1)} %copy.11) | copy-start | bytes 12582916
  396.1 2.2 copy-start.5
  398.3 36.5 %copy-start.7 = (f32[2,128,256]{2,1,0:T(8,128)S(1)}, f32[2,128,256]{2,1,0:T(8,128)}, u32[]{:S(2)}) copy-start(f32[2,128,256]{2,1,0:T(8,128)} %reduce-scatter.3.cloned.1.call-done) | copy-start | bytes 786436
Sparse Core Ops, SparseCore 0:
  10.2 25.6 all-gather.3
  45.7 103.7 all-reduce.2
  151.7 51.1 all-gather.5
  215.7 33.3 reduce-scatter.2
  251.2 22.0 all-gather.7
  283.1 103.7 all-reduce.4
  401.2 33.4 reduce-scatter.4
where the time goes:
time: 444 us; the launch traced here: 443 us
  waiting for transfers between devices  361 us (81%)
  local copies, waits for them, and re-layouts  24.7 us (6%)
  other arithmetic  21.6 us (5%)
  matrix products  21.4 us (5%)
  between operations  14.3 us (3%)
    psum x2, waiting for transfers between devices, local(): predicted = lax.psum(partial_value, 'col')  207 us
    reduce_scatter x2, waiting for transfers between devices, local(): lax.psum_scatter(gradient_part, 'row', scatter_dimension=1, tiled=True)  65.5 us
    all_gather x1, waiting for transfers between devices, local(): observed_block = lax.all_gather(observed, 'col', axis=1, tiled=True)  53.4 us
    all_gather x2, waiting for transfers between devices, local(): lax.all_gather(model.astype(jnp.bfloat16), 'row', axis=1, tiled=True)  34.6 us
    unnamed x22, local copies, waits for them, and re-layouts  21 us
    convert_element_type x2, other arithmetic, local(): misfit_half = full_misfit.astype(jnp.bfloat16)  10.5 us
    unnamed x4, matrix products  9.98 us
  transfers between devices with their start and end apart: 7, of which 7 were waited for; matrix products, arithmetic and copies ran while one was open for 4% of the time, Pallas kernels for 0%

commit v1 on v0

--- a/solution.py
+++ b/solution.py
@@ -47,7 +47,7 @@
             "fiajk,fijkl->fial", u_factors, coefficient, preferred_element_type=jnp.float32
         )
         partial_value = partial_value.reshape(frequencies, rows_here * tile_size, 2 * right_count)
-        predicted = lax.psum(partial_value, "col")
+        predicted = jnp.sum(lax.all_gather(partial_value, "col"), axis=0)
         full_misfit = predicted - observed_block
         misfit_half = full_misfit.astype(jnp.bfloat16)
         share = observed.shape[1]

time: 444 us -> 996 us (2.24)
  waiting for transfers between devices: 361 us -> 867 us
  other arithmetic: 21.6 us -> 67.9 us
    all_gather x0 -> x2, waiting for transfers between devices: none -> 736 us  [local(): predicted = jnp.sum(lax.all_gather(partial_value, 'col'), axis=0)]
    psum x2 -> x0, waiting for transfers between devices: 207 us -> none  [local(): predicted = lax.psum(partial_value, 'col')]
    reduce_sum x0 -> x2, other arithmetic: none -> 46.3 us  [local(): predicted = jnp.sum(lax.all_gather(partial_value, 'col'), axis=0)]
    all_gather x1, waiting for transfers between devices: 53.4 us -> 30 us  [local(): observed_block = lax.all_gather(observed, 'col', axis=1, tiled=True)]
where the time goes in v1:
time: 996 us
  waiting for transfers between devices  867 us (87%)
  other arithmetic  67.9 us (7%)
  local copies, waits for them, and re-layouts  24.7 us (2%)
  matrix products  21.4 us (2%)
  between operations  14.3 us (1%)
    all_gather x2, waiting for transfers between devices, local(): predicted = jnp.sum(lax.all_gather(partial_value, 'col'), axis=0)  736 us
    reduce_scatter x2, waiting for transfers between devices, local(): lax.psum_scatter(gradient_part, 'row', scatter_dimension=1, tiled=True)  65.4 us
    reduce_sum x2, other arithmetic, local(): predicted = jnp.sum(lax.all_gather(partial_value, 'col'), axis=0)  46.3 us
    all_gather x2, waiting for transfers between devices, local(): lax.all_gather(model.astype(jnp.bfloat16), 'row', axis=1, tiled=True)  34.6 us
    all_gather x1, waiting for transfers between devices, local(): observed_block = lax.all_gather(observed, 'col', axis=1, tiled=True)  30 us
    unnamed x22, local copies, waits for them, and re-layouts  21 us
  transfers between devices with their start and end apart: 7, of which 7 were waited for; matrix products, arithmetic and copies ran while one was open for 4% of the time, Pallas kernels for 0%

profile of v1, /device:TPU:0, one launch (start us, length us, event | category | flops | bytes accessed | tf_op | source)
XLA Modules:
  0.0 995.8 jit_solution(6100342334582928994)
XLA Ops:
  7.2 1.6 convert_element_type.23
  8.9 7.5 copy.20
  16.4 7.4 copy.23
  23.8 12.2 %all-gather.6.cloned.1.call-done = bf16[2,1024,256]{2,1,0:T(8,128)(2,1)} async-done(((bf16[2,128,256]{2,1,0:T(8,128)(2,1)}), bf16[2,1024,256]{2,1,0:T(8,128)(2,1)}) %all-gather.6.cloned.1.call-update) | async-done | bytes 1048592 | tf_op jit(solution)/shard_map/all_gather | solution.py:38
  36.0 3.7 fusion.49
  41.2 1.5 copy-done
  42.7 2.9 fusion.18
  46.4 367.9 %all-gather.8.cloned.1.call-done = f32[16,2,2048,256]{3,2,1,0:T(8,128)} async-done(((f32[1,2,2048,256]{3,2,1,0:T(8,128)}), f32[16,2,2048,256]{3,2,1,0:T(8,128)}) %all-gather.8.cloned.1.call-update) | async-done | bytes 67108880 | tf_op jit(solution)/shard_map/all_gather | solution.py:50
  414.3 23.3 %reduce_sum.18 = f32[2,2048,256]{2,1,0:T(8,128)} reduce(f32[16,2,2048,256]{3,2,1,0:T(8,128)} %all-gather.8.cloned.1.call-done, f32[]{:T(128)} %constant.2.clone.1), dimensions={0}, to_apply=%region_0.0 | reduce | flops 15728640 | bytes 71303168 | tf_op jit(solution)/shard_map/reduce_sum | solution.py:50
  437.7 30.0 %all-gather.10.cloned.1.call-done = f32[2,2048,256]{2,1,0:T(8,128)} async-done(((f32[2,128,256]{2,1,0:T(8,128)}), f32[2,2048,256]{2,1,0:T(8,128)}) %all-gather.10.cloned.1.call-update) | async-done | bytes 4194320 | tf_op jit(solution)/shard_map/all_gather | solution.py:36
  467.7 4.3 subtract_convert_fusion
  477.5 2.8 fusion
  480.4 33.5 %reduce-scatter.3.cloned.1.call-done = f32[2,128,256]{2,1,0:T(8,128)} async-done(((f32[2,1024,256]{2,1,0:T(8,128)}), f32[2,128,256]{2,1,0:T(8,128)}) %reduce-scatter.3.cloned.1.call-update) | async-done | bytes 262160 | tf_op jit(solution)/shard_map/reduce_scatter | solution.py:66
  513.9 1.7 fusion.36
  515.6 22.4 %all-gather.12.cloned.1.call-done = bf16[2,1024,256]{2,1,0:T(8,128)(2,1)} async-done(((bf16[2,128,256]{2,1,0:T(8,128)(2,1)}), bf16[2,1024,256]{2,1,0:T(8,128)(2,1)}) %all-gather.12.cloned.1.call-update) | async-done | bytes 1048592 | tf_op jit(solution)/shard_map/all_gather | solution.py:38
  538.1 3.7 fusion.51
  544.8 2.9 fusion.16
  547.9 368.5 %all-gather.14.cloned.1.call-done = f32[16,2,2048,256]{3,2,1,0:T(8,128)} async-done(((f32[1,2,2048,256]{3,2,1,0:T(8,128)}), f32[16,2,2048,256]{3,2,1,0:T(8,128)}) %all-gather.14.cloned.1.call-update) | async-done | bytes 67108880 | tf_op jit(solution)/shard_map/all_gather | solution.py:50
  916.4 22.9 %reduce_sum.19 = f32[2,2048,256]{2,1,0:T(8,128)} reduce(f32[16,2,2048,256]{3,2,1,0:T(8,128)} %all-gather.14.cloned.1.call-done, f32[]{:T(128)} %constant.2.clone.1), dimensions={0}, to_apply=%region_2.0 | reduce | flops 15728640 | bytes 71303168 | tf_op jit(solution)/shard_map/reduce_sum | solution.py:50
  939.4 6.2 fusion.42
  950.8 2.8 fusion.8
  953.6 1.7 constant_dynamic-slice_fusion
  955.3 31.9 %reduce-scatter.5.cloned.1.call-done = f32[2,128,256]{2,1,0:T(8,128)} async-done(((f32[2,1024,256]{2,1,0:T(8,128)}), f32[2,128,256]{2,1,0:T(8,128)}) %reduce-scatter.5.cloned.1.call-update) | async-done | bytes 262160 | tf_op jit(solution)/shard_map/reduce_scatter | solution.py:66
  987.2 1.8 multiply_subtract_fusion
  (46 shorter events, 16.5 us)
Async XLA Ops:
  7.2 28.8 %all-gather.6.cloned.1.call-start = ((), (), s32[]{:S(2)}) async-start(), calls=%async_computation.2 | async-start | bytes 1179648 | tf_op jit(solution)/shard_map/all_gather | solution.py:38
  8.9 405.5 %all-gather.8.cloned.1.call-start = ((), (), s32[]{:S(2)}) async-start(), calls=%async_computation.3 | async-start | bytes 71303168 | tf_op jit(solution)/shard_map/all_gather | solution.py:50
  16.4 7.4 copy-start.8
  40.5 2.2 copy-start
  45.6 422.0 %all-gather.10.cloned.1.call-start = ((), (), s32[]{:S(2)}) async-start(), calls=%async_computation.4 | async-start | bytes 4456448 | tf_op jit(solution)/shard_map/all_gather | solution.py:36
  46.4 467.5 %reduce-scatter.3.cloned.1.call-start = ((), (), s32[]{:S(2)}) async-start(), calls=%async_computation.5 | async-start | bytes 2359296 | tf_op jit(solution)/shard_map/reduce_scatter | solution.py:66
  467.7 4.6 copy-start.1
  475.3 2.2 copy-start.4
  477.5 36.3 %copy-start.6 = (f32[2,128,256]{2,1,0:T(8,128)S(1)}, f32[2,128,256]{2,1,0:T(8,128)}, u32[]{:S(2)}) copy-start(f32[2,128,256]{2,1,0:T(8,128)} %param.9) | copy-start | bytes 786436
  477.5 36.3 %copy-start.9 = (f32[2]{0:T(128)S(1)}, f32[2]{0:T(128)}, u32[]{:S(2)}) copy-start(f32[2]{0:T(128)} %param.11) | copy-start | bytes 28
  480.3 57.7 %all-gather.12.cloned.1.call-start = ((), (), s32[]{:S(2)}) async-start(), calls=%async_computation.6 | async-start | bytes 1179648 | tf_op jit(solution)/shard_map/all_gather | solution.py:38
  515.6 400.8 %all-gather.14.cloned.1.call-start = ((), (), s32[]{:S(2)}) async-start(), calls=%async_computation.7 | async-start | bytes 71303168 | tf_op jit(solution)/shard_map/all_gather | solution.py:50
  542.6 2.2 copy-start.2
  547.7 439.5 %reduce-scatter.5.cloned.1.call-start = ((), (), s32[]{:S(2)}) async-start(), calls=%async_computation.8 | async-start | bytes 2359296 | tf_op jit(solution)/shard_map/reduce_scatter | solution.py:66
  939.4 6.2 copy-start.3
  948.6 2.2 copy-start.5
  950.8 36.4 %copy-start.7 = (f32[2,128,256]{2,1,0:T(8,128)S(1)}, f32[2,128,256]{2,1,0:T(8,128)}, u32[]{:S(2)}) copy-start(f32[2,128,256]{2,1,0:T(8,128)} %reduce-scatter.3.cloned.1.call-done) | copy-start | bytes 786436
Sparse Core Ops, SparseCore 0:
  10.2 25.6 all-gather.5
  45.8 368.5 all-gather.7
  416.5 51.0 all-gather.9
  480.4 33.3 reduce-scatter.2
  516.0 22.0 all-gather.11
  547.8 368.5 all-gather.13
  953.7 33.4 reduce-scatter.4
